TPU v7x, 256 devices: a whole 4x4x8 slice. The times are simulated.
256 devices in a mesh: dp: 2 (over x_lo), expert: 128 (over y, z, x_hi, core).
Axes of the slice: x: 4 (x_hi: 2, x_lo: 2; x = x_hi * 2 + x_lo), y: 4, z: 8, core: 2. Of those that a mesh axis runs over, the one named last changes fastest.
Arguments:
- tokens: bfloat16 [256, 256, 1280], P(('dp', 'expert')), may hold values from -12 to 12
- router: bfloat16 [1280, 128], replicated, may hold values from -3 to 3
- w_in: bfloat16 [128, 1280, 5120], P('expert', None, 'dp'), may hold values from -0.15625 to 0.15625
- b_in: bfloat16 [128, 5120], P('expert'), may hold values from -3 to 3
- w_out: bfloat16 [128, 5120, 1280], P('expert', 'dp'), may hold values from -0.078125 to 0.078125
- b_out: bfloat16 [128, 1280], P('expert'), may hold values from -3 to 3
Outputs:
- mixed: bfloat16 [256, 256, 1280], P(('dp', 'expert'))
All inputs are finite; a program needn't handle non-finite values.
Results may differ from a plain program's by a relative error of at most 0.014.
Values may be sent and summed in bfloat16 or wider, within the bound.
A program may use at most 64 MiB of HBM per device.

v0:
```python
import jax
import jax.numpy as jnp
from jax import lax
from jax.sharding import Mesh
from jax.sharding import PartitionSpec as P

EXPERT = ("expert_0", "expert_1", "expert_2", "expert_3")
DP_EXPERT = ("dp", "expert_0", "expert_1", "expert_2", "expert_3")


def sent_to_all(shard, axis):
    copies = jnp.broadcast_to(shard, (lax.axis_size(axis), *shard.shape))
    return lax.all_to_all(copies, axis, split_axis=0, concat_axis=0, tiled=True)


def in_order(pieces, dim):
    pieces = jnp.moveaxis(pieces, 0, dim)
    dims = pieces.shape
    return pieces.reshape(*dims[:dim], dims[dim] * dims[dim + 1], *dims[dim + 2 :])


def gather_directly(shard, axis, dim):
    pieces = sent_to_all(shard, axis)
    return in_order(pieces, dim)


def in_blocks(shard, dim, count):
    dims = shard.shape
    pieces = shard.reshape(*dims[:dim], count, dims[dim] // count, *dims[dim + 1 :])
    return jnp.moveaxis(pieces, dim, 0)


def sent_and_summed(shard, axis, dim):
    pieces = in_blocks(shard, dim, lax.axis_size(axis))
    arrived = lax.all_to_all(pieces, axis, split_axis=0, concat_axis=0, tiled=True)
    return arrived.astype(jnp.float32).sum(axis=0)


def exchange_in_order(pieces, axes, turns):
    dims = [lax.axis_size(a) for a in axes]
    pieces = pieces.reshape(*dims, *pieces.shape[1:])
    for k in turns:
        pieces = lax.all_to_all(pieces, axes[k], split_axis=k, concat_axis=k, tiled=True)
    return pieces.reshape(-1, *pieces.shape[len(axes) :])


def two_step_exchange(shard, groups, turns, split_dim, concat_dim):
    count = lax.axis_size(groups[0]) * lax.axis_size(groups[1])
    pieces = in_blocks(shard, split_dim, count)
    return in_order(exchange_in_order(pieces, groups, turns), concat_dim)


def shards(tokens, router, w_in, b_in, w_out, b_out):
    logits = jnp.einsum("bmd,de->bme", tokens, router, preferred_element_type=jnp.float32)
    dispatch = jax.nn.softmax(logits, axis=1).astype(jnp.bfloat16)
    combine = jax.nn.softmax(logits, axis=2).astype(jnp.bfloat16)
    slot_inputs = jnp.einsum(
        "bme,bmd->ebd", dispatch, tokens, preferred_element_type=jnp.float32
    ).astype(jnp.bfloat16)
    width = tokens.shape[2]
    arrived = lax.all_to_all(slot_inputs, EXPERT, split_axis=0, concat_axis=0, tiled=True)
    sources = arrived.shape[0]
    images = arrived.shape[1]
    paired = gather_directly(arrived, "dp", 0)
    flat = paired.reshape(paired.shape[0] * images, width)
    half = w_in.shape[2]
    offset = lax.axis_index("dp") * half
    bias_half = lax.dynamic_slice_in_dim(b_in[0], offset, half, 0).astype(jnp.float32)
    hidden = jax.nn.gelu(
        jnp.dot(flat, w_in[0], preferred_element_type=jnp.float32) + bias_half, approximate=False
    ).astype(jnp.bfloat16)
    summed = sent_and_summed(
        jnp.dot(hidden, w_out[0], preferred_element_type=jnp.float32).astype(jnp.bfloat16), "dp", 0
    )
    result = (summed + b_out[0].astype(jnp.float32)).astype(jnp.bfloat16)
    shaped = result.reshape(sources, images, width)
    returned = two_step_exchange(
        shaped, (("expert_0", "expert_1", "expert_2"), "expert_3"), (1, 0), 0, 0
    )
    mixed = jnp.einsum("bme,ebd->bmd", combine, returned, preferred_element_type=jnp.float32)
    return mixed.astype(jnp.bfloat16)


def solution(mesh):
    finer = Mesh(
        mesh.devices.reshape(mesh.shape["dp"], 4, 8, 2, 2),
        ("dp", "expert_0", "expert_1", "expert_2", "expert_3"),
    )
    return jax.shard_map(
        shards,
        mesh=finer,
        in_specs=(
            P(DP_EXPERT, None, None),
            P(),
            P(EXPERT, None, "dp"),
            P(EXPERT, None),
            P(EXPERT, "dp", None),
            P(EXPERT, None),
        ),
        out_specs=P(DP_EXPERT, None, None),
        check_vma=False,
    )
```

profile of v0, /device:TPU:1, one launch (start us, length us, event | category | flops | bytes accessed | tf_op | source)
XLA Modules:
  0.0 103.0 jit_solution(1009964734027190072)
XLA Ops:
  0.0 0.0 copy-start
  0.0 1.1 %copy-done = bf16[1,256,1280]{2,1,0:T(8,128)(2,1)S(1)} copy-done((bf16[1,256,1280]{2,1,0:T(8,128)(2,1)S(1)}, bf16[1,256,1280]{2,1,0:T(8,128)(2,1)}, u32[]{:S(2)}) %copy-start) | copy-done | bytes 655384
  1.1 1.4 %fusion.97 = (f32[256]{0:T(256)S(1)}, f32[128]{0:T(128)S(1)}, f32[256,128]{1,0:T(8,128)S(1)}) fusion(bf16[1280,128]{1,0:T(8,128)(2,1)} %param.7, bf16[1,256,1280]{2,1,0:T(8,128)(2,1)S(1)} %copy-done), kind=kOutput, calls=%fused_computation.108 | convolution fusion | flops 83951232 | bytes 1115648 | tf_op jit(solution)/shard_map/bmd,de->bme/dot_general | solution.py:54
  2.5 0.2 fusion.61
  2.7 0.3 fusion.21
  3.0 0.5 broadcast.35
  3.5 0.8 reduce.12
  4.3 0.1 reshape.77
  4.4 0.0 copy-start.1
  4.4 33.2 %all_to_all.28 = bf16[128,2,640]{2,1,0:T(2,128)(2,1)S(1)} all-to-all(bf16[128,2,640]{2,1,0:T(2,128)(2,1)S(1)} %reshape.77), channel_id=1, replica_groups=mesh['dp'=2,'expert_0'=4,'expert_1'=8,'expert_2'=2,'expert_3'=2] {'exper..., dimensions={0} | all-to-all | bytes 655360 | tf_op jit(solution)/shard_map/all_to_all | solution.py:61
  37.6 0.3 reshape.78
  37.9 0.9 broadcast_in_dim.2
  38.8 3.5 %all-to-all-start.1 = ((bf16[2,128,1,1280]{3,1,2,0:T(8,128)(2,1)}), bf16[2,128,1,1280]{3,1,2,0:T(8,128)(2,1)S(1)}, u32[]{:S(2)}, u32[]{:S(2)}) async-start(bf16[2,128,1,1280]{3,1,2,0:T(8,128)(2,1)} %broadcast_in_dim.2), calls=%async_computation.1 | async-start | bytes 1310720 | tf_op jit(solution)/shard_map/all_to_all | solution.py:13
  42.4 9.3 %all-to-all-done.1 = bf16[2,128,1,1280]{3,1,2,0:T(8,128)(2,1)S(1)} async-done(((bf16[2,128,1,1280]{3,1,2,0:T(8,128)(2,1)}), bf16[2,128,1,1280]{3,1,2,0:T(8,128)(2,1)S(1)}, u32[]{:S(2)}, u32[]{:S(2)}) %all-to-all-start.1) | async-done | bytes 655392 | tf_op jit(solution)/shard_map/all_to_all | solution.py:13
  51.7 14.1 %fusion.17 = bf16[256,1280]{1,0:T(8,128)(2,1)} fusion(bf16[1,2560,1280]{2,1,0:T(8,128)(2,1)} %param.10, bf16[256,1280]{1,0:T(8,128)(2,1)S(1)} %bitcast.40, bf16[1,1280,2560]{2,1,0:T(8,128)(2,1)} %param.8, f32[2560]{0:T(1024)S(1)} %convert_reduce_fusion.1), kind=kOutput, calls=%fused_computation.24 | convolution fusion | flops 3399024640 | bytes 14428160 | tf_op jit(solution)/shard_map/dot_general | solution.py:73
  65.8 3.5 %all-to-all-start.2 = ((bf16[2,128,1280]{2,1,0:T(8,128)(2,1)}), bf16[2,128,1280]{2,1,0:T(8,128)(2,1)S(1)}, u32[]{:S(2)}, u32[]{:S(2)}) async-start(bf16[2,128,1280]{2,1,0:T(8,128)(2,1)} %bitcast.7), calls=%async_computation.2 | async-start | bytes 1310720 | tf_op jit(solution)/shard_map/all_to_all | solution.py:35
  69.3 8.4 %all-to-all-done.2 = bf16[2,128,1280]{2,1,0:T(8,128)(2,1)S(1)} async-done(((bf16[2,128,1280]{2,1,0:T(8,128)(2,1)}), bf16[2,128,1280]{2,1,0:T(8,128)(2,1)S(1)}, u32[]{:S(2)}, u32[]{:S(2)}) %all-to-all-start.2) | async-done | bytes 655392 | tf_op jit(solution)/shard_map/all_to_all | solution.py:35
  77.8 0.1 convert_reduce_fusion
  77.9 0.4 reduce_sum.32
  78.3 5.5 %all_to_all.29 = bf16[64,2,1,1,1280]{4,0,3,2,1:T(8,128)(2,1)S(1)} all-to-all(bf16[64,2,1,1,1280]{4,0,3,2,1:T(8,128)(2,1)S(1)} %fusion.60), channel_id=1, replica_groups=mesh['dp'=2,'expert_0'=4,'expert_1'=8,'expert_2'=2,'expert_3'=2] {'exper..., dimensions={1} | all-to-all | bytes 655360 | tf_op jit(solution)/shard_map/all_to_all | solution.py:43
  83.8 0.3 copy.14
  84.1 17.5 %all_to_all.30 = bf16[64,2,1,1,1280]{4,1,3,2,0:T(2,128)(2,1)S(1)} all-to-all(bf16[64,2,1,1,1280]{4,1,3,2,0:T(2,128)(2,1)S(1)} %copy.14), channel_id=1, replica_groups=mesh['dp'=2,'expert_0'=4,'expert_1'=8,'expert_2'=2,'expert_3'=2] {'exper..., dimensions={0} | all-to-all | bytes 655360 | tf_op jit(solution)/shard_map/all_to_all | solution.py:43
  101.6 0.1 reshape.72
  101.8 1.2 %fusion.20 = bf16[1,256,1280]{2,1,0:T(8,128)(2,1)} fusion(bf16[128,1280]{1,0:T(8,128)(2,1)S(1)} %reshape.72, f32[256,128]{1,0:T(8,128)S(1)} %get-tuple-element.9, f32[256]{0:T(256)S(1)} %get-tuple-element.5, f32[256]{0:T(256)S(1)} %get-tuple-element.7), kind=kOutput, calls=%fused_computation.26 | convolution fusion | flops 84312064 | bytes 1116160 | tf_op jit(solution)/shard_map/bme,ebd->bmd/dot_general | solution.py:80
  (7 shorter events, 0.1 us)
Async XLA Ops:
  0.0 1.1 %copy-start = (bf16[1,256,1280]{2,1,0:T(8,128)(2,1)S(1)}, bf16[1,256,1280]{2,1,0:T(8,128)(2,1)}, u32[]{:S(2)}) copy-start(bf16[1,256,1280]{2,1,0:T(8,128)(2,1)} %param.6) | copy-start | bytes 1966084
  4.4 38.0 %copy-start.1 = (bf16[1,5120]{1,0:T(2,128)(2,1)S(1)}, bf16[1,5120]{1,0:T(2,128)(2,1)}, u32[]{:S(2)}) copy-start(bf16[1,5120]{1,0:T(2,128)(2,1)} %param.9) | copy-start | bytes 30724
  38.8 12.9 %all-to-all-start.1 = ((bf16[2,128,1,1280]{3,1,2,0:T(8,128)(2,1)}), bf16[2,128,1,1280]{3,1,2,0:T(8,128)(2,1)S(1)}, u32[]{:S(2)}, u32[]{:S(2)}) async-start(bf16[2,128,1,1280]{3,1,2,0:T(8,128)(2,1)} %broadcast_in_dim.2), calls=%async_computation.1 | async-start | bytes 1310720 | tf_op jit(solution)/shard_map/all_to_all | solution.py:13
  51.7 17.6 %copy-start.2 = (bf16[1,1280]{1,0:T(2,128)(2,1)S(1)}, bf16[1,1280]{1,0:T(2,128)(2,1)}, u32[]{:S(2)}) copy-start(bf16[1,1280]{1,0:T(2,128)(2,1)} %param.11) | copy-start | bytes 7684
  65.8 12.0 %all-to-all-start.2 = ((bf16[2,128,1280]{2,1,0:T(8,128)(2,1)}), bf16[2,128,1280]{2,1,0:T(8,128)(2,1)S(1)}, u32[]{:S(2)}, u32[]{:S(2)}) async-start(bf16[2,128,1280]{2,1,0:T(8,128)(2,1)} %bitcast.7), calls=%async_computation.2 | async-start | bytes 1310720 | tf_op jit(solution)/shard_map/all_to_all | solution.py:35
where the time goes:
time: 103 us
  blocking collectives  56.2 us (55%)
  waiting for transfers between devices  17.7 us (17%)
  matrix products  17 us (17%)
  starting transfers between devices  7.02 us (7%)
  local copies, waits for them, and re-layouts  3.72 us (4%)
  other arithmetic  1.24 us (1%)
    all_to_all x1, blocking collectives, shards(): lax.all_to_all(slot_inputs, EXPERT, split_axis=0, concat_axis=0, tiled=True)  33.2 us
    all_to_all x2, blocking collectives, exchange_in_order(): lax.all_to_all(pieces, axes[k], split_axis=k, concat_axis=k, tiled=True)  22.9 us
    dot_general x1, matrix products, shards(): jnp.dot(hidden, w_out[0], preferred_element_type=jnp.float32)  14.1 us
    all_to_all x1, waiting for transfers between devices, sent_to_all(): return lax.all_to_all(copies, axis, split_axis=0, concat_axis=0, tiled=True)  9.29 us
    all_to_all x1, waiting for transfers between devices, sent_and_summed(): lax.all_to_all(pieces, axis, split_axis=0, concat_axis=0, tiled=True)  8.45 us
    all_to_all x1, starting transfers between devices, sent_to_all(): return lax.all_to_all(copies, axis, split_axis=0, concat_axis=0, tiled=True)  3.51 us
    all_to_all x1, starting transfers between devices, sent_and_summed(): lax.all_to_all(pieces, axis, split_axis=0, concat_axis=0, tiled=True)  3.51 us
  transfers between devices with their start and end apart: 2, of which 2 were waited for; matrix products, arithmetic and copies ran while one was open for 0% of the time, Pallas kernels for 0%

commit v1 on v0

v1 whole, which is shorter than its diff:
```python
import functools
import jax
import jax.numpy as jnp
from jax import lax
from jax.experimental import pallas as pl
from jax.experimental.pallas import tpu as pltpu
from jax.sharding import Mesh
from jax.sharding import PartitionSpec as P

AXES = ("dp", "y", "z", "xh", "core")
EXPERT = ("y", "z", "xh", "core")
F32 = jnp.float32
BF16 = jnp.bfloat16
LOGICAL = pl.DeviceIdType.LOGICAL
NY, NZ = 4, 8
EXPERTS = 128
HALF = 640
BATCH = 64
GROUP = 16
SLOTS = [(dy, dz, dx, dc) for dy in range(NY) for dz in range(NZ) for dx in range(2) for dc in range(2)]


def hops(place):
    dy, dz, dx, _ = place
    return min(dy, NY - dy) + min(dz, NZ - dz) + dx


def one_hot(shape, col_of_row):
    rows = lax.broadcasted_iota(jnp.int32, shape, 0)
    cols = lax.broadcasted_iota(jnp.int32, shape, 1)
    return jnp.where(cols == col_of_row(rows), 1.0, 0.0).astype(BF16)


def spread(shape, h):
    rows = lax.broadcasted_iota(jnp.int32, shape, 0)
    cols = lax.broadcasted_iota(jnp.int32, shape, 1)
    return jnp.where(cols == 2 * rows + h, 1.0, 0.0).astype(BF16)


def spread_t(shape, h):
    rows = lax.broadcasted_iota(jnp.int32, shape, 0)
    cols = lax.broadcasted_iota(jnp.int32, shape, 1)
    return jnp.where(rows == 2 * cols + h, 1.0, 0.0).astype(BF16)


def dot(a, b):
    return jnp.dot(a, b, preferred_element_type=F32)


def dot_nt(a, b):
    return lax.dot_general(a, b, (((1,), (1,)), ((), ())), preferred_element_type=F32)


def gelu(v):
    return v * (1.0 + lax.erf(v * 0.7071067811865476)) * 0.5


def kernel(
    tokens_h, router_h, w_in_h, b_in_h, w_out_h, b_out_h, out_ref,
    tok, router, w_in, w_out, b_in, b_out, src, got, got2, x, hidden, part, psend, precv, rsrc, ret, comb2, self2, unit,
    load_sem, w_sem, send_sem, recv_sem, fsend_sem, frecv_sem, psend_sem, precv_sem, rsend_sem, rrecv_sem,
):
    dp, y, z, xh, c = (lax.axis_index(a) for a in AXES)
    ys = [lax.rem(y + k, NY) * 32 for k in range(NY)]
    zs = [lax.rem(z + k, NZ) * 4 for k in range(NZ)]
    xs = [xh * 2, (1 - xh) * 2]
    cs = [c, 1 - c]
    ds = [dp * EXPERTS, (1 - dp) * EXPERTS]
    me = ys[0] + zs[0] + xs[0] + cs[0]
    partner = me + ds[1]

    def expert_at(place, sign=1):
        dy, dz, dx, dc = place
        return ys[(sign * dy) % NY] + zs[(sign * dz) % NZ] + xs[dx] + cs[dc]

    def device_at(place, sign=1):
        return expert_at(place, sign) + ds[place[2]]

    half = w_in.shape[1]
    loads = [
        pltpu.make_async_copy(tokens_h.at[0], tok, load_sem.at[0]),
        pltpu.make_async_copy(router_h, router, load_sem.at[1]),
        pltpu.make_async_copy(b_in_h.at[:, pl.ds(pl.multiple_of(dp * half, half), half)], b_in, load_sem.at[2]),
        pltpu.make_async_copy(b_out_h, b_out, load_sem.at[3]),
    ]
    weights = [
        pltpu.make_async_copy(w_in_h.at[0], w_in, w_sem.at[0]),
        pltpu.make_async_copy(w_out_h.at[0], w_out, w_sem.at[1]),
    ]
    for copy in loads[:2]:
        copy.start()
    ret[...] = jnp.zeros_like(ret)

    barrier = pltpu.get_barrier_semaphore()
    for place in sorted(SLOTS[1:], key=hops, reverse=True):
        pl.semaphore_signal(barrier, inc=1, device_id=device_at(place), device_id_type=LOGICAL)
    pl.semaphore_signal(barrier, inc=1, device_id=partner, device_id_type=LOGICAL)
    for copy in loads[2:] + weights:
        copy.start()

    for copy in loads[:2]:
        copy.wait()
    logits = dot(tok[...], router[...])
    up = jnp.exp(logits - jnp.max(logits, axis=0, keepdims=True))
    dispatch = (up / jnp.sum(up, axis=0, keepdims=True)).astype(BF16)
    across = jnp.exp(logits - jnp.max(logits, axis=1, keepdims=True))
    combine = (across / jnp.sum(across, axis=1, keepdims=True)).astype(BF16)
    rows = None
    for h in range(2):
        lhs = dot_nt(spread_t((2 * EXPERTS, EXPERTS), h), dispatch).astype(BF16)
        term = dot(lhs, tok[:, h * HALF : (h + 1) * HALF])
        rows = term if rows is None else rows + term
        comb2[h] = dot(combine, spread((EXPERTS, 2 * EXPERTS), h)).astype(BF16)
        pick = lax.broadcasted_iota(jnp.int32, (EXPERTS, 2 * BATCH), 0) == me
        into = lax.broadcasted_iota(jnp.int32, (EXPERTS, 2 * BATCH), 1) == h
        self2[h] = dot(combine, jnp.where(pick & into, 1.0, 0.0).astype(BF16)).astype(BF16)
    src[...] = rows.astype(BF16)
    mine = dot(one_hot((8, 2 * EXPERTS), lambda r: 2 * me + r), src[...]).astype(BF16)
    got[0:2, :] = mine[0:2, :]

    pl.semaphore_wait(barrier, len(SLOTS))

    for k, place in enumerate(SLOTS):
        if k == 0:
            continue
        pltpu.make_async_remote_copy(
            src.at[pl.ds(pl.multiple_of(2 * expert_at(place), 2), 2)],
            got.at[pl.ds(2 * k, 2)],
            send_sem, recv_sem.at[k // GROUP],
            device_id=device_at(place), device_id_type=LOGICAL,
        ).start()

    def forward(g):
        held = unit.at[pl.ds(0, GROUP - 1 if g == 0 else GROUP)]
        pltpu.make_async_copy(held, held, recv_sem.at[g]).wait()
        block = pl.ds(2 * GROUP * g, 2 * GROUP)
        pltpu.make_async_remote_copy(
            got.at[block], got2.at[block], fsend_sem, frecv_sem.at[2 * GROUP * g // (2 * BATCH)],
            device_id=partner, device_id_type=LOGICAL,
        ).start()

    groups = EXPERTS // GROUP
    width = w_in.shape[0]

    def first_half(b):
        block = pl.ds(2 * BATCH * b, 2 * BATCH)
        pltpu.make_async_copy(got2.at[block], got2.at[block], frecv_sem.at[b]).wait()
        for h in range(2):
            order = spread((BATCH, 2 * BATCH), h)
            x[0:BATCH, h * HALF : (h + 1) * HALF] = dot(order, got[block, :]).astype(BF16)
            x[BATCH : 2 * BATCH, h * HALF : (h + 1) * HALF] = dot(order, got2[block, :]).astype(BF16)
        if b == 0:
            loads[2].wait()
            weights[0].wait()
        step = 512
        for j in range(half // step):
            cols = slice(j * step, (j + 1) * step)
            acc = dot(x[...], w_in[:, cols]) + b_in[:, cols].astype(F32)
            hidden[:, cols] = gelu(acc).astype(BF16)

    def second_half(b):
        if b == 0:
            weights[1].wait()
        step = 256
        for j in range(width // step):
            cols = slice(j * step, (j + 1) * step)
            acc = dot(hidden[...], w_out[:, cols])
            part[b, :, cols] = acc[0:BATCH]
            psend[b, :, cols] = acc[BATCH : 2 * BATCH].astype(BF16)
        pltpu.make_async_remote_copy(
            psend.at[b], precv.at[b], psend_sem, precv_sem.at[b], device_id=partner, device_id_type=LOGICAL
        ).start()

    def send_back(b):
        pltpu.make_async_copy(precv.at[b], precv.at[b], precv_sem.at[b]).wait()
        if b == 0:
            loads[3].wait()
        result = (part[b] + precv[b].astype(F32) + b_out[...].astype(F32)).astype(BF16)
        rows = None
        for h in range(2):
            term = dot(spread_t((2 * BATCH, BATCH), h), result[:, h * HALF : (h + 1) * HALF])
            rows = term if rows is None else rows + term
        rsrc[b] = rows.astype(BF16)
        for i in range(BATCH):
            k = BATCH * b + i
            if k == 0:
                continue
            pltpu.make_async_remote_copy(
                rsrc.at[b, pl.ds(2 * i, 2)],
                ret.at[pl.ds(pl.multiple_of(2 * me, 2), 2)],
                rsend_sem, rrecv_sem,
                device_id=device_at(SLOTS[k], -1), device_id_type=LOGICAL,
            ).start()

    for g in range(groups // 2):
        forward(g)
    first_half(0)
    for g in range(groups // 2, groups):
        forward(g)
    second_half(0)
    first_half(1)
    send_back(0)
    second_half(1)
    send_back(1)

    others = unit.at[pl.ds(0, EXPERTS - 1)]
    pltpu.make_async_copy(others, others, rrecv_sem).wait()
    for h in range(2):
        mixed = dot(comb2[h], ret[...]) + dot(self2[h], rsrc[0])
        out_ref[:, h * HALF : (h + 1) * HALF] = mixed.astype(BF16)

    pltpu.make_async_copy(others, others, send_sem).wait()
    pltpu.make_async_copy(others, others, rsend_sem).wait()
    pltpu.make_async_copy(got, got, fsend_sem).wait()
    pltpu.make_async_copy(psend, psend, psend_sem).wait()


def layer(tokens, router, w_in, b_in, w_out, b_out):
    _, m, d = tokens.shape
    half = w_in.shape[2]
    anywhere = pl.BlockSpec(memory_space=pl.ANY)
    dma = pltpu.SemaphoreType.DMA
    out = pl.pallas_call(
        kernel,
        name="soft_moe",
        out_shape=jax.ShapeDtypeStruct((m, d), BF16),
        in_specs=[anywhere] * 6,
        out_specs=pl.BlockSpec(memory_space=pltpu.VMEM),
        scratch_shapes=[
            pltpu.VMEM((m, d), BF16),
            pltpu.VMEM((d, EXPERTS), BF16),
            pltpu.VMEM((d, half), BF16),
            pltpu.VMEM((half, d), BF16),
            pltpu.VMEM((1, half), BF16),
            pltpu.VMEM((1, d), BF16),
            pltpu.VMEM((2 * EXPERTS, HALF), BF16),
            pltpu.VMEM((2 * EXPERTS, HALF), BF16),
            pltpu.VMEM((2 * EXPERTS, HALF), BF16),
            pltpu.VMEM((2 * BATCH, d), BF16),
            pltpu.VMEM((2 * BATCH, half), BF16),
            pltpu.VMEM((2, BATCH, d), F32),
            pltpu.VMEM((2, BATCH, d), BF16),
            pltpu.VMEM((2, BATCH, d), BF16),
            pltpu.VMEM((2, 2 * BATCH, HALF), BF16),
            pltpu.VMEM((2 * EXPERTS, HALF), BF16),
            pltpu.VMEM((2, m, 2 * EXPERTS), BF16),
            pltpu.VMEM((2, m, 2 * BATCH), BF16),
            pltpu.VMEM((EXPERTS, 2, HALF), BF16),
            dma((4,)), dma((2,)),
            dma, dma((EXPERTS // GROUP,)),
            dma, dma((2,)),
            dma, dma((2,)),
            dma, dma,
        ],
        compiler_params=pltpu.CompilerParams(
            collective_id=1, has_side_effects=True, vmem_limit_bytes=48 * 1024 * 1024
        ),
    )(tokens, router, w_in, b_in, w_out, b_out)
    return out[None]


def solution(mesh):
    finer = Mesh(mesh.devices.reshape(mesh.shape["dp"], NY, NZ, 2, 2), AXES)
    return jax.shard_map(
        layer,
        mesh=finer,
        in_specs=(
            P(AXES, None, None),
            P(),
            P(EXPERT, None, "dp"),
            P(EXPERT, None),
            P(EXPERT, "dp", None),
            P(EXPERT, None),
        ),
        out_specs=P(AXES, None, None),
        check_vma=False,
    )
```

time: 103 us -> 53.8 us (0.52)
  blocking collectives: 56.2 us -> 0 us
  Pallas kernels: 0 us -> 49.2 us
  waiting for transfers between devices: 17.7 us -> 0 us
  matrix products: 17 us -> 0 us
  starting transfers between devices: 7.02 us -> 0 us
  other arithmetic: 1.24 us -> 0 us
    all_to_all x3 -> x0, blocking collectives: 56.2 us -> none  [the longest x1 33.2 us: shards(): lax.all_to_all(slot_inputs, EXPERT, split_axis=0, concat_axis=0, tiled=True)]
    pallas_call x0 -> x1, Pallas kernels: none -> 49.2 us  [layer(): pl.pallas_call(kernel, name='soft_moe', out_shape=jax.ShapeDtypeStruct((m...]
    all_to_all x2 -> x0, waiting for transfers between devices: 17.7 us -> none  [the longest x1 9.29 us: sent_to_all(): return lax.all_to_all(copies, axis, split_axis=0, concat_axis=0, tiled=True)]
    dot_general x4 -> x0, matrix products: 17 us -> none  [the longest x1 14.1 us: shards(): jnp.dot(hidden, w_out[0], preferred_element_type=jnp.float32)]
    all_to_all x2 -> x0, starting transfers between devices: 7.02 us -> none  [the longest x1 3.51 us: sent_to_all(): return lax.all_to_all(copies, axis, split_axis=0, concat_axis=0, tiled=True)]
    unnamed x9, local copies, waits for them, and re-layouts: 1.48 us -> 4.31 us
  transfers between devices with their start and end apart: 2 -> 0, of which waited for: 2 -> 0; matrix products, arithmetic and copies ran while one was open for 0% -> 0% of each run, Pallas kernels for 0% -> 0%
where the time goes in v1:
time: 53.8 us; the launch traced here: 53.5 us
  Pallas kernels  49.2 us (91%)
  local copies, waits for them, and re-layouts  4.31 us (8%)
    pallas_call x1, Pallas kernels, layer(): pl.pallas_call(kernel, name='soft_moe', out_shape=jax.ShapeDtypeStruct((m...  49.2 us
    unnamed x9, local copies, waits for them, and re-layouts  4.31 us

profile of v1, /device:TPU:1, one launch (start us, length us, event | category | flops | bytes accessed | tf_op | source)
XLA Modules:
  0.0 53.5 jit_solution(4901633808498120699)
XLA Ops:
  0.0 0.0 copy-start
  0.0 1.1 %copy-done = bf16[1,256,1280]{2,1,0:T(8,128)(2,1)S(1)} copy-done((bf16[1,256,1280]{2,1,0:T(8,128)(2,1)S(1)}, bf16[1,256,1280]{2,1,0:T(8,128)(2,1)}, u32[]{:S(2)}) %copy-start) | copy-done | bytes 655384
  1.1 0.0 copy-start.1
  1.1 1.0 %copy-done.1 = bf16[1280,128]{1,0:T(8,128)(2,1)S(1)} copy-done((bf16[1280,128]{1,0:T(8,128)(2,1)S(1)}, bf16[1280,128]{1,0:T(8,128)(2,1)}, u32[]{:S(2)}) %copy-start.1) | copy-done | bytes 327704
  2.1 0.0 copy-start.2
  2.1 0.7 %copy-done.2 = bf16[1,5120]{1,0:T(2,128)(2,1)S(1)} copy-done((bf16[1,5120]{1,0:T(2,128)(2,1)S(1)}, bf16[1,5120]{1,0:T(2,128)(2,1)}, u32[]{:S(2)}) %copy-start.2) | copy-done | bytes 10264
  2.8 0.0 copy-start.3
  2.8 0.7 %copy-done.3 = bf16[1,1280]{1,0:T(2,128)(2,1)S(1)} copy-done((bf16[1,1280]{1,0:T(2,128)(2,1)S(1)}, bf16[1,1280]{1,0:T(2,128)(2,1)}, u32[]{:S(2)}) %copy-start.3) | copy-done | bytes 2584
  3.5 49.2 %soft_moe.1 = bf16[256,1280]{1,0:T(8,128)(2,1)S(1)} custom-call(bf16[1,256,1280]{2,1,0:T(8,128)(2,1)S(1)} %copy-done, bf16[1280,128]{1,0:T(8,128)(2,1)S(1)} %copy-done.1, bf16[1,1280,2560]{2,1,0:T(8,128)(2,1)} %w_in_h.1, bf16[1,5120]{1,0:T(2,128)(2,1)S(1)} %copy-done.2, bf16[1,2560,1280]{2,1,0:T(8,128)(2,1)} %w_out_h.1, bf16[1,1280]{1,0:T(2,128)(2,1)S(1)} %copy-done.3), custom_call_target="tpu_custom_call" | custom-call | tf_op jit(solution)/shard_map/soft_moe/pallas_call | solution.py:223
  52.7 0.8 %copy.8 = bf16[1,256,1280]{2,1,0:T(8,128)(2,1)} copy(bf16[1,256,1280]{2,1,0:T(8,128)(2,1)S(1)} %bitcast.1) | data formatting | bytes 1310720
Async XLA Ops:
  0.0 1.1 %copy-start = (bf16[1,256,1280]{2,1,0:T(8,128)(2,1)S(1)}, bf16[1,256,1280]{2,1,0:T(8,128)(2,1)}, u32[]{:S(2)}) copy-start(bf16[1,256,1280]{2,1,0:T(8,128)(2,1)} %tokens_h.1) | copy-start | bytes 1966084
  1.1 1.0 %copy-start.1 = (bf16[1280,128]{1,0:T(8,128)(2,1)S(1)}, bf16[1280,128]{1,0:T(8,128)(2,1)}, u32[]{:S(2)}) copy-start(bf16[1280,128]{1,0:T(8,128)(2,1)} %router_h.1) | copy-start | bytes 983044
  2.1 0.7 %copy-start.2 = (bf16[1,5120]{1,0:T(2,128)(2,1)S(1)}, bf16[1,5120]{1,0:T(2,128)(2,1)}, u32[]{:S(2)}) copy-start(bf16[1,5120]{1,0:T(2,128)(2,1)} %b_in_h.1) | copy-start | bytes 30724
  2.8 0.7 %copy-start.3 = (bf16[1,1280]{1,0:T(2,128)(2,1)S(1)}, bf16[1,1280]{1,0:T(2,128)(2,1)}, u32[]{:S(2)}) copy-start(bf16[1,1280]{1,0:T(2,128)(2,1)} %b_out_h.1) | copy-start | bytes 7684

commit v2 on v1

--- a/solution.py
+++ b/solution.py
@@ -15,15 +15,27 @@
 NY, NZ = 4, 8
 EXPERTS = 128
 HALF = 640
-BATCH = 64
-GROUP = 16
-SLOTS = [(dy, dz, dx, dc) for dy in range(NY) for dz in range(NZ) for dx in range(2) for dc in range(2)]
 
 
 def hops(place):
     dy, dz, dx, _ = place
     return min(dy, NY - dy) + min(dz, NZ - dz) + dx
 
+
+PLACES = sorted(
+    ((dy, dz, dx, dc) for dy in range(NY) for dz in range(NZ) for dx in range(2) for dc in range(2)), key=hops
+)
+ORDER = "O1"
+SLOTS = {
+    "O1": PLACES,
+    "O2": PLACES[::-1],
+    "O3": PLACES[:32] + PLACES[96:] + PLACES[64:96] + PLACES[32:64],
+    "O4": sorted(PLACES),
+}[ORDER]
+SELF = SLOTS.index((0, 0, 0, 0))
+SIZES = (32, 32, 32, 32)
+BATCHES = [(sum(SIZES[:b]), n) for b, n in enumerate(SIZES)]
+SCHEDULE = "F0 F1 G0 H0 F2 G1 H1 R0 F3 G2 H2 R1 G3 H3 R2 R3"
 
 def one_hot(shape, col_of_row):
     rows = lax.broadcasted_iota(jnp.int32, shape, 0)
@@ -98,6 +110,7 @@
     for copy in loads[2:] + weights:
         copy.start()
 
+    self_block, self_row = 2 * SELF // EXPERTS, 2 * SELF % EXPERTS
     for copy in loads[:2]:
         copy.wait()
     logits = dot(tok[...], router[...])
@@ -111,102 +124,98 @@
         term = dot(lhs, tok[:, h * HALF : (h + 1) * HALF])
         rows = term if rows is None else rows + term
         comb2[h] = dot(combine, spread((EXPERTS, 2 * EXPERTS), h)).astype(BF16)
-        pick = lax.broadcasted_iota(jnp.int32, (EXPERTS, 2 * BATCH), 0) == me
-        into = lax.broadcasted_iota(jnp.int32, (EXPERTS, 2 * BATCH), 1) == h
+        pick = lax.broadcasted_iota(jnp.int32, (EXPERTS, EXPERTS), 0) == me
+        into = lax.broadcasted_iota(jnp.int32, (EXPERTS, EXPERTS), 1) == self_row + h
         self2[h] = dot(combine, jnp.where(pick & into, 1.0, 0.0).astype(BF16)).astype(BF16)
     src[...] = rows.astype(BF16)
     mine = dot(one_hot((8, 2 * EXPERTS), lambda r: 2 * me + r), src[...]).astype(BF16)
-    got[0:2, :] = mine[0:2, :]
+    got[2 * SELF : 2 * SELF + 2, :] = mine[0:2, :]
 
     pl.semaphore_wait(barrier, len(SLOTS))
 
-    for k, place in enumerate(SLOTS):
-        if k == 0:
-            continue
+    for b, (first, count) in enumerate(BATCHES):
+        for k in range(first, first + count):
+            if k != SELF:
+                pltpu.make_async_remote_copy(
+                    src.at[pl.ds(pl.multiple_of(2 * expert_at(SLOTS[k]), 2), 2)],
+                    got.at[pl.ds(2 * k, 2)],
+                    send_sem, recv_sem.at[b],
+                    device_id=device_at(SLOTS[k]), device_id_type=LOGICAL,
+                ).start()
+
+    width = w_in.shape[0]
+
+    def forward(b):
+        first, count = BATCHES[b]
+        held = unit.at[pl.ds(0, count - 1 if first <= SELF < first + count else count)]
+        pltpu.make_async_copy(held, held, recv_sem.at[b]).wait()
+        block = pl.ds(2 * first, 2 * count)
         pltpu.make_async_remote_copy(
-            src.at[pl.ds(pl.multiple_of(2 * expert_at(place), 2), 2)],
-            got.at[pl.ds(2 * k, 2)],
-            send_sem, recv_sem.at[k // GROUP],
-            device_id=device_at(place), device_id_type=LOGICAL,
+            got.at[block], got2.at[block], fsend_sem, frecv_sem.at[b], device_id=partner, device_id_type=LOGICAL
         ).start()
 
-    def forward(g):
-        held = unit.at[pl.ds(0, GROUP - 1 if g == 0 else GROUP)]
-        pltpu.make_async_copy(held, held, recv_sem.at[g]).wait()
-        block = pl.ds(2 * GROUP * g, 2 * GROUP)
-        pltpu.make_async_remote_copy(
-            got.at[block], got2.at[block], fsend_sem, frecv_sem.at[2 * GROUP * g // (2 * BATCH)],
-            device_id=partner, device_id_type=LOGICAL,
-        ).start()
-
-    groups = EXPERTS // GROUP
-    width = w_in.shape[0]
-
     def first_half(b):
-        block = pl.ds(2 * BATCH * b, 2 * BATCH)
+        first, count = BATCHES[b]
+        block = pl.ds(2 * first, 2 * count)
         pltpu.make_async_copy(got2.at[block], got2.at[block], frecv_sem.at[b]).wait()
         for h in range(2):
-            order = spread((BATCH, 2 * BATCH), h)
-            x[0:BATCH, h * HALF : (h + 1) * HALF] = dot(order, got[block, :]).astype(BF16)
-            x[BATCH : 2 * BATCH, h * HALF : (h + 1) * HALF] = dot(order, got2[block, :]).astype(BF16)
+            order = spread((count, 2 * count), h)
+            x[0:count, h * HALF : (h + 1) * HALF] = dot(order, got[block, :]).astype(BF16)
+            x[count : 2 * count, h * HALF : (h + 1) * HALF] = dot(order, got2[block, :]).astype(BF16)
         if b == 0:
             loads[2].wait()
             weights[0].wait()
         step = 512
         for j in range(half // step):
             cols = slice(j * step, (j + 1) * step)
-            acc = dot(x[...], w_in[:, cols]) + b_in[:, cols].astype(F32)
-            hidden[:, cols] = gelu(acc).astype(BF16)
+            acc = dot(x[0 : 2 * count], w_in[:, cols]) + b_in[:, cols].astype(F32)
+            hidden[0 : 2 * count, cols] = gelu(acc).astype(BF16)
 
     def second_half(b):
+        first, count = BATCHES[b]
+        block = pl.ds(first, count)
         if b == 0:
             weights[1].wait()
         step = 256
         for j in range(width // step):
             cols = slice(j * step, (j + 1) * step)
-            acc = dot(hidden[...], w_out[:, cols])
-            part[b, :, cols] = acc[0:BATCH]
-            psend[b, :, cols] = acc[BATCH : 2 * BATCH].astype(BF16)
+            acc = dot(hidden[0 : 2 * count], w_out[:, cols])
+            part[block, cols] = acc[0:count]
+            psend[block, cols] = acc[count : 2 * count].astype(BF16)
         pltpu.make_async_remote_copy(
-            psend.at[b], precv.at[b], psend_sem, precv_sem.at[b], device_id=partner, device_id_type=LOGICAL
+            psend.at[block], precv.at[block], psend_sem, precv_sem.at[b], device_id=partner, device_id_type=LOGICAL
         ).start()
 
     def send_back(b):
-        pltpu.make_async_copy(precv.at[b], precv.at[b], precv_sem.at[b]).wait()
+        first, count = BATCHES[b]
+        block = pl.ds(first, count)
+        pltpu.make_async_copy(precv.at[block], precv.at[block], precv_sem.at[b]).wait()
         if b == 0:
             loads[3].wait()
-        result = (part[b] + precv[b].astype(F32) + b_out[...].astype(F32)).astype(BF16)
+        result = (part[block, :] + precv[block, :].astype(F32) + b_out[...].astype(F32)).astype(BF16)
         rows = None
         for h in range(2):
-            term = dot(spread_t((2 * BATCH, BATCH), h), result[:, h * HALF : (h + 1) * HALF])
+            term = dot(spread_t((2 * count, count), h), result[:, h * HALF : (h + 1) * HALF])
             rows = term if rows is None else rows + term
-        rsrc[b] = rows.astype(BF16)
-        for i in range(BATCH):
-            k = BATCH * b + i
-            if k == 0:
-                continue
-            pltpu.make_async_remote_copy(
-                rsrc.at[b, pl.ds(2 * i, 2)],
-                ret.at[pl.ds(pl.multiple_of(2 * me, 2), 2)],
-                rsend_sem, rrecv_sem,
-                device_id=device_at(SLOTS[k], -1), device_id_type=LOGICAL,
-            ).start()
-
-    for g in range(groups // 2):
-        forward(g)
-    first_half(0)
-    for g in range(groups // 2, groups):
-        forward(g)
-    second_half(0)
-    first_half(1)
-    send_back(0)
-    second_half(1)
-    send_back(1)
+        rsrc[pl.ds(2 * first, 2 * count), :] = rows.astype(BF16)
+        for k in range(first, first + count):
+            if k != SELF:
+                pltpu.make_async_remote_copy(
+                    rsrc.at[pl.ds(2 * k, 2)],
+                    ret.at[pl.ds(pl.multiple_of(2 * me, 2), 2)],
+                    rsend_sem, rrecv_sem,
+                    device_id=device_at(SLOTS[k], -1), device_id_type=LOGICAL,
+                ).start()
+
+    stages = {"F": forward, "G": first_half, "H": second_half, "R": send_back}
+    for stage in SCHEDULE.split():
+        stages[stage[0]](int(stage[1:]))
 
     others = unit.at[pl.ds(0, EXPERTS - 1)]
     pltpu.make_async_copy(others, others, rrecv_sem).wait()
     for h in range(2):
-        mixed = dot(comb2[h], ret[...]) + dot(self2[h], rsrc[0])
+        own = rsrc[self_block * EXPERTS : (self_block + 1) * EXPERTS, :]
+        mixed = dot(comb2[h], ret[...]) + dot(self2[h], own)
         out_ref[:, h * HALF : (h + 1) * HALF] = mixed.astype(BF16)
 
     pltpu.make_async_copy(others, others, send_sem).wait()
@@ -218,7 +227,7 @@
 def layer(tokens, router, w_in, b_in, w_out, b_out):
     _, m, d = tokens.shape
     half = w_in.shape[2]
-    anywhere = pl.BlockSpec(memory_space=pl.ANY)
+    anywhere = pl.BlockSpec(memory_space=pltpu.HBM)
     dma = pltpu.SemaphoreType.DMA
     out = pl.pallas_call(
         kernel,
@@ -236,24 +245,24 @@
             pltpu.VMEM((2 * EXPERTS, HALF), BF16),
             pltpu.VMEM((2 * EXPERTS, HALF), BF16),
             pltpu.VMEM((2 * EXPERTS, HALF), BF16),
-            pltpu.VMEM((2 * BATCH, d), BF16),
-            pltpu.VMEM((2 * BATCH, half), BF16),
-            pltpu.VMEM((2, BATCH, d), F32),
-            pltpu.VMEM((2, BATCH, d), BF16),
-            pltpu.VMEM((2, BATCH, d), BF16),
-            pltpu.VMEM((2, 2 * BATCH, HALF), BF16),
+            pltpu.VMEM((2 * max(SIZES), d), BF16),
+            pltpu.VMEM((2 * max(SIZES), half), BF16),
+            pltpu.VMEM((EXPERTS, d), F32),
+            pltpu.VMEM((EXPERTS, d), BF16),
+            pltpu.VMEM((EXPERTS, d), BF16),
+            pltpu.VMEM((2 * EXPERTS, HALF), BF16),
             pltpu.VMEM((2 * EXPERTS, HALF), BF16),
             pltpu.VMEM((2, m, 2 * EXPERTS), BF16),
-            pltpu.VMEM((2, m, 2 * BATCH), BF16),
+            pltpu.VMEM((2, m, EXPERTS), BF16),
             pltpu.VMEM((EXPERTS, 2, HALF), BF16),
             dma((4,)), dma((2,)),
-            dma, dma((EXPERTS // GROUP,)),
-            dma, dma((2,)),
-            dma, dma((2,)),
+            dma, dma((len(SIZES),)),
+            dma, dma((len(SIZES),)),
+            dma, dma((len(SIZES),)),
             dma, dma,
         ],
         compiler_params=pltpu.CompilerParams(
-            collective_id=1, has_side_effects=True, vmem_limit_bytes=48 * 1024 * 1024
+            collective_id=1, has_side_effects=True, vmem_limit_bytes=67043328
         ),
     )(tokens, router, w_in, b_in, w_out, b_out)
     return out[None]

time: 53.8 us -> 50 us (0.929)
  local copies, waits for them, and re-layouts: 4.31 us -> 1.97 us
  Pallas kernels: 49.2 us -> 47.9 us
    unnamed x9 -> x1, local copies, waits for them, and re-layouts: 4.31 us -> 1.97 us
    pallas_call x1, Pallas kernels: 49.2 us -> 47.9 us  [layer(): pl.pallas_call(kernel, name='soft_moe', out_shape=jax.ShapeDtypeStruct((m...]
where the time goes in v2:
time: 50 us; the launch traced here: 49.9 us
  Pallas kernels  47.9 us (96%)
  local copies, waits for them, and re-layouts  1.97 us (4%)
    pallas_call x1, Pallas kernels, layer(): pl.pallas_call(kernel, name='soft_moe', out_shape=jax.ShapeDtypeStruct((m...  47.9 us
    unnamed x1, local copies, waits for them, and re-layouts  1.97 us

profile of v2, /device:TPU:1, one launch (start us, length us, event | category | flops | bytes accessed | tf_op | source)
XLA Modules:
  0.0 49.9 jit_solution(11493428065464156027)
XLA Ops:
  0.0 47.9 %soft_moe.1 = bf16[256,1280]{1,0:T(8,128)(2,1)} custom-call(bf16[1,256,1280]{2,1,0:T(8,128)(2,1)} %tokens_h.1, bf16[1280,128]{1,0:T(8,128)(2,1)} %router_h.1, bf16[1,1280,2560]{2,1,0:T(8,128)(2,1)} %w_in_h.1, bf16[1,5120]{1,0:T(2,128)(2,1)} %b_in_h.1, bf16[1,2560,1280]{2,1,0:T(8,128)(2,1)} %w_out_h.1, bf16[1,1280]{1,0:T(2,128)(2,1)} %b_out_h.1), custom_call_target="tpu_custom_call" | custom-call | tf_op jit(solution)/shard_map/soft_moe/pallas_call | solution.py:232
  47.9 2.0 %copy.8 = bf16[1,256,1280]{2,1,0:T(8,128)(2,1)} copy(bf16[1,256,1280]{2,1,0:T(8,128)(2,1)} %bitcast.1) | data formatting | bytes 1310720

commit v3 on v2

--- a/solution.py
+++ b/solution.py
@@ -31,11 +31,13 @@
     "O2": PLACES[::-1],
     "O3": PLACES[:32] + PLACES[96:] + PLACES[64:96] + PLACES[32:64],
     "O4": sorted(PLACES),
+    "O5": PLACES[:64] + PLACES[96:] + PLACES[64:96],
+    "O6": PLACES[:32] + PLACES[64:] + PLACES[32:64],
 }[ORDER]
 SELF = SLOTS.index((0, 0, 0, 0))
 SIZES = (32, 32, 32, 32)
 BATCHES = [(sum(SIZES[:b]), n) for b, n in enumerate(SIZES)]
-SCHEDULE = "F0 F1 G0 H0 F2 G1 H1 R0 F3 G2 H2 R1 G3 H3 R2 R3"
+SCHEDULE = ("F0", "F1", "G0", "F2", "H0", "F3", "G1", "H1", "G2", "R0", "H2", "G3", "R1", "H3", "R2", "R3")
 
 def one_hot(shape, col_of_row):
     rows = lax.broadcasted_iota(jnp.int32, shape, 0)
@@ -208,7 +210,7 @@
                 ).start()
 
     stages = {"F": forward, "G": first_half, "H": second_half, "R": send_back}
-    for stage in SCHEDULE.split():
+    for stage in SCHEDULE:
         stages[stage[0]](int(stage[1:]))
 
     others = unit.at[pl.ds(0, EXPERTS - 1)]

time: 50 us -> 49 us (0.980)
  Pallas kernels: 47.9 us -> 46.9 us
    pallas_call x1, Pallas kernels: 47.9 us -> 46.9 us  [layer(): pl.pallas_call(kernel, name='soft_moe', out_shape=jax.ShapeDtypeStruct((m...]
where the time goes in v3:
time: 49 us; the launch traced here: 48.8 us
  Pallas kernels  46.9 us (96%)
  local copies, waits for them, and re-layouts  1.97 us (4%)
    pallas_call x1, Pallas kernels, layer(): pl.pallas_call(kernel, name='soft_moe', out_shape=jax.ShapeDtypeStruct((m...  46.9 us
    unnamed x1, local copies, waits for them, and re-layouts  1.97 us

profile of v3, /device:TPU:1, one launch (start us, length us, event | category | flops | bytes accessed | tf_op | source)
XLA Modules:
  0.0 48.8 jit_solution(3452038886159968836)
XLA Ops:
  0.0 46.9 %soft_moe.1 = bf16[256,1280]{1,0:T(8,128)(2,1)} custom-call(bf16[1,256,1280]{2,1,0:T(8,128)(2,1)} %tokens_h.1, bf16[1280,128]{1,0:T(8,128)(2,1)} %router_h.1, bf16[1,1280,2560]{2,1,0:T(8,128)(2,1)} %w_in_h.1, bf16[1,5120]{1,0:T(2,128)(2,1)} %b_in_h.1, bf16[1,2560,1280]{2,1,0:T(8,128)(2,1)} %w_out_h.1, bf16[1,1280]{1,0:T(2,128)(2,1)} %b_out_h.1), custom_call_target="tpu_custom_call" | custom-call | tf_op jit(solution)/shard_map/soft_moe/pallas_call | solution.py:234
  46.9 2.0 %copy.8 = bf16[1,256,1280]{2,1,0:T(8,128)(2,1)} copy(bf16[1,256,1280]{2,1,0:T(8,128)(2,1)} %bitcast.1) | data formatting | bytes 1310720
